TPU v7x, 32 devices: a whole 2x2x4 slice. The times are simulated.
32 devices in a mesh: trial: 4 (over z), ep: 4 (over y, core), fsdp: 2 (over x).
Axes of the slice: x: 2, y: 2, z: 4, core: 2. Of those that a mesh axis runs over, the one named last changes fastest.
Arguments:
- master_down: float32 [256, 1024, 2048], P(('trial', 'ep'), None, 'fsdp'), parts along dimension 0, may hold values from -0.25 to 0.25
- router_weight: float32 [8192, 64], P(('trial', 'fsdp'), 'ep'), parts along dimension 0, may hold values from -0.125 to 0.125
- router_gain: float32 [8192], P(('trial', 'fsdp')), parts along dimension 0, may hold values from 0.25 to 1.75
Outputs:
- final_down: bfloat16 [256, 1024, 2048], P(('trial', 'ep'), 'fsdp'), parts along dimension 0
- scale_down: float32 [256, 1024], P(('trial', 'ep'), 'fsdp'), parts along dimension 0
- serve_router: bfloat16 [8192, 64], P('trial'), parts along dimension 0
There are 4 independent parts, one for each index of `trial`. A program takes and returns all parts, laid end to end along the dimension named above; each array names one. Nothing has to cross between parts.
All inputs are finite; a program needn't handle non-finite values. Where the computation divides by a largest or mean magnitude, that divisor is 1e-20 or more.
Results may differ from a plain program's by a relative error of at most 0.001.
Values may be sent and summed in bfloat16 or wider, within the bound.
A program may use at most 256 MiB of HBM per device.

v0:
```python
import jax
import jax.numpy as jnp
from jax import lax
from jax.sharding import PartitionSpec as P


def shards(master_down, router_weight, router_gain):
    scale_down = lax.pmax(jnp.max(jnp.abs(master_down), axis=2), "fsdp")
    narrow_down = (master_down / jnp.expand_dims(scale_down, 2)).astype(jnp.bfloat16)
    final_down = lax.all_to_all(narrow_down, "fsdp", split_axis=1, concat_axis=2, tiled=True)
    scale_down = lax.dynamic_slice_in_dim(
        scale_down, lax.axis_index("fsdp") * final_down.shape[1], final_down.shape[1], axis=1
    )
    part_router = (router_weight * router_gain[:, None]).astype(jnp.bfloat16)
    row_router = lax.all_gather(part_router, "fsdp", axis=0, tiled=True)
    serve_router = lax.all_gather(row_router, "ep", axis=1, tiled=True)
    return (final_down, scale_down, serve_router)


def solution(mesh):
    return jax.shard_map(
        shards,
        mesh=mesh,
        in_specs=(
            P(("trial", "ep"), None, "fsdp"),
            P(("trial", "fsdp"), "ep"),
            P(("trial", "fsdp")),
        ),
        out_specs=(P(("trial", "ep"), "fsdp", None), P(("trial", "ep"), "fsdp"), P("trial", None)),
        check_vma=False,
    )
```

profile of v0, /device:TPU:0, one launch (start us, length us, event | category | flops | bytes accessed | tf_op | source)
XLA Modules:
  0.0 617.7 jit_solution(5879946227713915781)
XLA Ops:
  7.2 0.0 all-reduce.2.cloned.1.call-start
  7.2 21.4 %abs_reduce_fusion = f32[16,1024]{1,0:T(8,128)} fusion(f32[16,1024,1024]{2,1,0:T(8,128)} %param.3), kind=kLoop, calls=%fused_computation.2 | loop fusion | flops 33538048 | bytes 67174400 | tf_op jit(solution)/shard_map/reduce_max | solution.py:8
  28.6 0.0 all-reduce.2.cloned.1.call-update
  28.6 23.8 %all-reduce.2.cloned.1.call-done = f32[16,1024]{1,0:T(8,128)} async-done(((f32[16,1024]{1,0:T(8,128)}), f32[16,1024]{1,0:T(8,128)}) %all-reduce.2.cloned.1.call-update) | async-done | bytes 65552 | tf_op jit(solution)/shard_map/pmax | solution.py:8
  52.5 1.0 copy.7
  53.5 0.0 copy-start.1
  53.5 0.0 copy-start.2
  53.5 0.0 copy-start
  53.6 60.1 %fusion = bf16[16,1024,1024]{2,0,1:T(8,128)(2,1)} fusion(f32[16,1024,1024]{2,1,0:T(8,128)} %param.3, f32[16,1024]{0,1:T(8,128)S(1)} %copy.7), kind=kLoop, calls=%fused_computation.1 | loop fusion | flops 33554432 | bytes 100728832 | tf_op jit(solution)/shard_map/convert_element_type | solution.py:9
  113.7 13.0 %all-to-all-start = ((bf16[16,1024,1024]{2,0,1:T(8,128)(2,1)}), bf16[16,1024,1024]{2,0,1:T(8,128)(2,1)}, u32[]{:S(2)}, u32[]{:S(2)}) async-start(bf16[16,1024,1024]{2,0,1:T(8,128)(2,1)} %fusion), calls=%async_computation | async-start | bytes 67108864 | tf_op jit(solution)/shard_map/all_to_all | solution.py:10
  126.7 0.0 copy-done.1
  126.7 0.0 copy-done.2
  126.7 362.4 %all_gather.6 = bf16[2048,16]{0,1:T(8,128)(2,1)S(1)} all-gather(bf16[1024,16]{0,1:T(8,128)(2,1)S(1)} %multiply_convert_fusion), channel_id=1, replica_groups=mesh['trial'=4,'ep'=4,'fsdp'=2] {'fsdp'}, dimensions={0}, use_global_device_ids=true | all-gather | bytes 98304 | tf_op jit(solution)/shard_map/all_gather | solution.py:15
  489.1 5.8 all_gather.7
  494.8 0.0 copy-done
  494.8 0.6 constant_dynamic-slice_fusion
  495.4 0.0 all-to-all-done
  495.5 60.5 %copy.9 = bf16[16,512,2,1024]{3,2,1,0:T(2,128)(2,1)} copy(bf16[16,512,2,1024]{3,0,1,2:T(8,128)(2,1)} %bitcast.1) | data formatting | bytes 67108864 | tf_op jit(solution)/shard_map/all_to_all | solution.py:10
  556.0 54.2 %all_to_all.16 = bf16[16,512,2048]{2,1,0:T(8,128)(2,1)} reshape(bf16[16,512,2,1024]{3,2,1,0:T(2,128)(2,1)} %copy.9) | data formatting | bytes 67108864 | tf_op jit(solution)/shard_map/all_to_all | solution.py:10
  610.2 0.7 copy.15
  (1 shorter events, 0.0 us)
Async XLA Ops:
  7.2 45.3 %all-reduce.2.cloned.1.call-start = ((), (), s32[]{:S(2)}) async-start(), calls=%async_computation.1 | async-start | bytes 131072 | tf_op jit(solution)/shard_map/pmax | solution.py:8
  53.5 73.1 %copy-start.1 = (f32[1024,16]{0,1:T(8,128)S(1)}, f32[1024,16]{0,1:T(8,128)}, u32[]{:S(2)}) copy-start(f32[1024,16]{0,1:T(8,128)} %param.4) | copy-start | bytes 196612
  53.5 73.1 %copy-start.2 = (f32[1024]{0:T(1024)S(1)}, f32[1024]{0:T(1024)}, u32[]{:S(2)}) copy-start(f32[1024]{0:T(1024)} %param.5) | copy-start | bytes 12292
  53.5 441.3 %copy-start = (f32[16,1024]{1,0:T(8,128)S(1)}, f32[16,1024]{1,0:T(8,128)}, u32[]{:S(2)}) copy-start(f32[16,1024]{1,0:T(8,128)} %all-reduce.2.cloned.1.call-done) | copy-start | bytes 196612
  113.7 381.8 %all-to-all-start = ((bf16[16,1024,1024]{2,0,1:T(8,128)(2,1)}), bf16[16,1024,1024]{2,0,1:T(8,128)(2,1)}, u32[]{:S(2)}, u32[]{:S(2)}) async-start(bf16[16,1024,1024]{2,0,1:T(8,128)(2,1)} %fusion), calls=%async_computation | async-start | bytes 67108864 | tf_op jit(solution)/shard_map/all_to_all | solution.py:10
Sparse Core Ops, SparseCore 0:
  28.8 23.6 all-reduce.1
where the time goes:
time: 619 us; the launch traced here: 618 us
  blocking collectives  368 us (59%)
  local copies, waits for them, and re-layouts  117 us (19%)
  other arithmetic  81.6 us (13%)
  waiting for transfers between devices  23.9 us (4%)
  between operations  14.1 us (2%)
  starting transfers between devices  13 us (2%)
    all_gather x1, blocking collectives, shards(): row_router = lax.all_gather(part_router, 'fsdp', axis=0, tiled=True)  362 us
    all_to_all x2, local copies, waits for them, and re-layouts, shards(): lax.all_to_all(narrow_down, 'fsdp', split_axis=1, concat_axis=2, tiled=True)  115 us
    convert_element_type x1, other arithmetic, shards(): (master_down / jnp.expand_dims(scale_down, 2)).astype(jnp.bfloat16)  60.1 us
    pmax x1, waiting for transfers between devices, shards(): scale_down = lax.pmax(jnp.max(jnp.abs(master_down), axis=2), 'fsdp')  23.8 us
    reduce_max x1, other arithmetic, shards(): scale_down = lax.pmax(jnp.max(jnp.abs(master_down), axis=2), 'fsdp')  21.4 us
    all_to_all x1, starting transfers between devices, shards(): lax.all_to_all(narrow_down, 'fsdp', split_axis=1, concat_axis=2, tiled=True)  13 us
  transfers between devices with their start and end apart: 2, of which 1 were waited for; matrix products, arithmetic and copies ran while one was open for 0% of the time, Pallas kernels for 0%

commit v1 on v0

--- a/solution.py
+++ b/solution.py
@@ -4,10 +4,16 @@
 from jax.sharding import PartitionSpec as P
 
 
+def swap_blocks(x, axis, split, join):
+    pieces = jnp.split(x, lax.axis_size(axis), axis=split)
+    incoming = lax.all_to_all(jnp.stack(pieces), axis, 0, 0)
+    return jnp.concatenate(incoming, axis=join)
+
+
 def shards(master_down, router_weight, router_gain):
     scale_down = lax.pmax(jnp.max(jnp.abs(master_down), axis=2), "fsdp")
     narrow_down = (master_down / jnp.expand_dims(scale_down, 2)).astype(jnp.bfloat16)
-    final_down = lax.all_to_all(narrow_down, "fsdp", split_axis=1, concat_axis=2, tiled=True)
+    final_down = swap_blocks(narrow_down, "fsdp", 1, 2)
     scale_down = lax.dynamic_slice_in_dim(
         scale_down, lax.axis_index("fsdp") * final_down.shape[1], final_down.shape[1], axis=1
     )

time: 619 us -> 544 us (0.88)
  local copies, waits for them, and re-layouts: 117 us -> 47.7 us
    all_to_all x2 -> x0, local copies, waits for them, and re-layouts: 115 us -> none  [shards(): lax.all_to_all(narrow_down, 'fsdp', split_axis=1, concat_axis=2, tiled=True)]
    convert_element_type x1, other arithmetic: 60.1 us -> 32.9 us  [shards(): (master_down / jnp.expand_dims(scale_down, 2)).astype(jnp.bfloat16)]
    reshape x0 -> x1, local copies, waits for them, and re-layouts: none -> 23.3 us  [swap_blocks(): return jnp.concatenate(incoming, axis=join)]
    another operation x0 -> x1, local copies, waits for them, and re-layouts: none -> 23.1 us  [swap_blocks(): incoming = lax.all_to_all(jnp.stack(pieces), axis, 0, 0)]
    another operation x0 -> x1, other arithmetic: none -> 23 us  [swap_blocks(): incoming = lax.all_to_all(jnp.stack(pieces), axis, 0, 0)]
where the time goes in v1:
time: 544 us
  blocking collectives  368 us (68%)
  other arithmetic  77.3 us (14%)
  local copies, waits for them, and re-layouts  47.7 us (9%)
  waiting for transfers between devices  23.9 us (4%)
  between operations  14.1 us (3%)
  starting transfers between devices  13.1 us (2%)
    all_gather x1, blocking collectives, shards(): row_router = lax.all_gather(part_router, 'fsdp', axis=0, tiled=True)  362 us
    convert_element_type x1, other arithmetic, shards(): (master_down / jnp.expand_dims(scale_down, 2)).astype(jnp.bfloat16)  32.9 us
    pmax x1, waiting for transfers between devices, shards(): scale_down = lax.pmax(jnp.max(jnp.abs(master_down), axis=2), 'fsdp')  23.8 us
    reshape x1, local copies, waits for them, and re-layouts, swap_blocks(): return jnp.concatenate(incoming, axis=join)  23.3 us
    another operation x1, local copies, waits for them, and re-layouts, swap_blocks(): incoming = lax.all_to_all(jnp.stack(pieces), axis, 0, 0)  23.1 us
    another operation x1, other arithmetic, swap_blocks(): incoming = lax.all_to_all(jnp.stack(pieces), axis, 0, 0)  23 us
    reduce_max x1, other arithmetic, shards(): scale_down = lax.pmax(jnp.max(jnp.abs(master_down), axis=2), 'fsdp')  21.4 us
    all_to_all x1, starting transfers between devices, swap_blocks(): incoming = lax.all_to_all(jnp.stack(pieces), axis, 0, 0)  13.1 us
  transfers between devices with their start and end apart: 2, of which 1 were waited for; matrix products, arithmetic and copies ran while one was open for 0% of the time, Pallas kernels for 0%

profile of v1, /device:TPU:0, one launch (start us, length us, event | category | flops | bytes accessed | tf_op | source)
XLA Modules:
  0.0 544.2 jit_solution(12114528892555993120)
XLA Ops:
  7.2 0.0 all-reduce.2.cloned.1.call-start
  7.2 21.4 %abs_reduce_fusion = f32[16,1024]{1,0:T(8,128)} fusion(f32[16,1024,1024]{2,1,0:T(8,128)} %param.3), kind=kLoop, calls=%fused_computation.1 | loop fusion | flops 33538048 | bytes 67174400 | tf_op jit(solution)/shard_map/reduce_max | solution.py:14
  28.6 0.0 all-reduce.2.cloned.1.call-update
  28.6 23.8 %all-reduce.2.cloned.1.call-done = f32[16,1024]{1,0:T(8,128)} async-done(((f32[16,1024]{1,0:T(8,128)}), f32[16,1024]{1,0:T(8,128)}) %all-reduce.2.cloned.1.call-update) | async-done | bytes 65552 | tf_op jit(solution)/shard_map/pmax | solution.py:14
  52.5 32.9 %divide_convert_fusion = bf16[16,1024,1024]{2,1,0:T(8,128)(2,1)} fusion(f32[16,1024,1024]{2,1,0:T(8,128)} %param.3, f32[16,1024]{1,0:T(8,128)} %all-reduce.2.cloned.1.call-done), kind=kLoop, calls=%fused_computation | loop fusion | flops 33554432 | bytes 100728832 | tf_op jit(solution)/shard_map/convert_element_type | solution.py:15
  85.4 23.1 %slice_bitcast_fusion.1 = (bf16[1,16,512,1024]{3,2,1,0:T(8,128)(2,1)}, bf16[1,16,512,1024]{3,2,1,0:T(8,128)(2,1)}) fusion(bf16[16,1024,1024]{2,1,0:T(8,128)(2,1)} %divide_convert_fusion), kind=kLoop, calls=%fused_computation.4 | loop fusion | bytes 67108864 | tf_op jit(solution)/shard_map/stack | solution.py:9
  108.5 23.0 %pad_maximum_fusion = bf16[2,16,512,1024]{3,2,1,0:T(8,128)(2,1)} fusion(bf16[1,16,512,1024]{3,2,1,0:T(8,128)(2,1)} %get-tuple-element.4, bf16[1,16,512,1024]{3,2,1,0:T(8,128)(2,1)} %get-tuple-element.3), kind=kLoop, calls=%fused_computation.2 | loop fusion | flops 16777216 | bytes 67108864 | tf_op jit(solution)/shard_map/stack | solution.py:9
  131.4 0.0 copy-start.1
  131.4 0.0 copy-start.2
  131.5 0.0 copy-start
  131.5 13.1 %all-to-all-start = ((bf16[2,16,512,1024]{3,2,1,0:T(8,128)(2,1)}), bf16[2,16,512,1024]{3,2,1,0:T(8,128)(2,1)}, u32[]{:S(2)}, u32[]{:S(2)}) async-start(bf16[2,16,512,1024]{3,2,1,0:T(8,128)(2,1)} %pad_maximum_fusion), calls=%async_computation | async-start | bytes 67108864 | tf_op jit(solution)/shard_map/all_to_all | solution.py:9
  144.6 0.0 copy-done.1
  144.6 0.0 copy-done.2
  144.6 362.4 %all_gather.6 = bf16[2048,16]{0,1:T(8,128)(2,1)S(1)} all-gather(bf16[1024,16]{0,1:T(8,128)(2,1)S(1)} %multiply_convert_fusion), channel_id=1, replica_groups=mesh['trial'=4,'ep'=4,'fsdp'=2] {'fsdp'}, dimensions={0}, use_global_device_ids=true | all-gather | bytes 98304 | tf_op jit(solution)/shard_map/all_gather | solution.py:21
  507.0 5.8 %all_gather.7 = bf16[2048,64]{0,1:T(8,128)(2,1)S(1)} all-gather(bf16[2048,16]{0,1:T(8,128)(2,1)S(1)} %all_gather.6), channel_id=1, replica_groups=mesh['trial'=4,'ep'=4,'fsdp'=2] {'ep'}, dimensions={1}, use_global_device_ids=true | all-gather | bytes 327680 | tf_op jit(solution)/shard_map/all_gather | solution.py:22
  512.7 0.0 copy-done
  512.7 0.6 constant_dynamic-slice_fusion
  513.4 0.0 all-to-all-done
  513.4 23.3 %copy.7 = bf16[2,16,64,8,1024]{4,3,0,2,1:T(8,128)(2,1)} copy(bf16[2,16,64,8,1024]{4,3,2,1,0:T(8,128)(2,1)} %bitcast.3) | data formatting | bytes 67108864 | tf_op jit(solution)/shard_map/reshape | solution.py:10
  536.6 0.7 copy.10
  (1 shorter events, 0.0 us)
Async XLA Ops:
  7.2 45.3 %all-reduce.2.cloned.1.call-start = ((), (), s32[]{:S(2)}) async-start(), calls=%async_computation.1 | async-start | bytes 131072 | tf_op jit(solution)/shard_map/pmax | solution.py:14
  131.4 13.2 %copy-start.1 = (f32[1024,16]{0,1:T(8,128)S(1)}, f32[1024,16]{0,1:T(8,128)}, u32[]{:S(2)}) copy-start(f32[1024,16]{0,1:T(8,128)} %param.4) | copy-start | bytes 196612
  131.4 13.2 %copy-start.2 = (f32[1024]{0:T(1024)S(1)}, f32[1024]{0:T(1024)}, u32[]{:S(2)}) copy-start(f32[1024]{0:T(1024)} %param.5) | copy-start | bytes 12292
  131.5 381.3 %copy-start = (f32[16,1024]{1,0:T(8,128)S(1)}, f32[16,1024]{1,0:T(8,128)}, u32[]{:S(2)}) copy-start(f32[16,1024]{1,0:T(8,128)} %all-reduce.2.cloned.1.call-done) | copy-start | bytes 196612
  131.5 381.9 %all-to-all-start = ((bf16[2,16,512,1024]{3,2,1,0:T(8,128)(2,1)}), bf16[2,16,512,1024]{3,2,1,0:T(8,128)(2,1)}, u32[]{:S(2)}, u32[]{:S(2)}) async-start(bf16[2,16,512,1024]{3,2,1,0:T(8,128)(2,1)} %pad_maximum_fusion), calls=%async_computation | async-start | bytes 67108864 | tf_op jit(solution)/shard_map/all_to_all | solution.py:9
Sparse Core Ops, SparseCore 0:
  28.8 23.6 all-reduce.1
